TPU v7x, 32 devices: a whole 2x2x4 slice. The times are simulated.
32 devices in a mesh: grp: 2 (over y), col: 4 (over z), slc: 2 (over x), bat: 2 (over core).
Axes of the slice: x: 2, y: 2, z: 4, core: 2. Of those that a mesh axis runs over, the one named last changes fastest.
Arguments:
- site_tensors: bfloat16 [4, 72, 2, 64, 128], P(('grp', 'slc'), 'col'), parts along dimension 0, may hold values from -1.2 to 1.2
- left_edge: float32 [4, 64, 128], P(('grp', 'slc')), parts along dimension 0, may hold values from -0.5 to 0.5
- right_edge: float32 [4, 64, 128], P(('grp', 'slc')), parts along dimension 0, may hold values from -0.5 to 0.5
- order: int32 [144], P(('grp', 'col')), parts along dimension 0, may hold values from 0 to 71, each once
- bitstrings: int32 [128, 72], P(('grp', 'bat')), parts along dimension 0, may hold values 0 or 1
Outputs:
- amplitudes: float32 [2, 128], P(None, ('grp', 'bat')), parts along dimension 1
There are 2 independent parts, one for each index of `grp`. A program takes and returns all parts, laid end to end along the dimension named above; each array names one. Nothing has to cross between parts.
Inputs may be any that keep to these rules, and one draw needn't show every extreme that they name: `order`: a permutation of the 72 qubit indices.
All inputs are finite; a program needn't handle non-finite values. No bound on the sum of `bitstrings` on one device may be relied on, other than what follows from the above.
Results may differ from a plain program's by a relative error of at most 0.0003.
Values sent between devices are 32-bit elements; how exact they have to be, the bound alone decides.
A program may use at most 64 MiB of HBM per device.

v0:
```python
import jax
import jax.numpy as jnp
from jax import lax
from jax.sharding import PartitionSpec as P


def rotate(block):
    middle = block.shape[-1] // 2
    return jnp.concatenate([-block[..., middle:], block[..., :middle]], axis=-1)


def complex_product(first_factor, second_factor):
    stacked = jnp.concatenate([second_factor, rotate(second_factor)], axis=-2)
    return jnp.einsum("bij,bjk->bik", first_factor, stacked, precision=lax.Precision.HIGHEST)


def closing(boundary, edge):
    middle = boundary.shape[-1] // 2
    real_left = boundary[..., :middle]
    imag_left = boundary[..., middle:]
    real_right = edge[..., :middle]
    imag_right = edge[..., middle:]
    real_part = jnp.sum(real_left * real_right - imag_left * imag_right, axis=(1, 2))
    imag_part = jnp.sum(real_left * imag_right + imag_left * real_right, axis=(1, 2))
    return jnp.stack([real_part, imag_part])


def select_site(tensors, site_bits, position):
    matrices = lax.dynamic_index_in_dim(tensors, position, 0, keepdims=False)
    chosen_bits = lax.dynamic_index_in_dim(site_bits, position, 1, keepdims=False)
    return jnp.where(chosen_bits[:, None, None] == 1, matrices[1], matrices[0])


def column_product(tensors, site_bits):
    site_count = tensors.shape[0]
    leading = select_site(tensors, site_bits, 0)
    return lax.fori_loop(
        1,
        site_count,
        lambda position, carried: complex_product(
            carried, select_site(tensors, site_bits, position)
        ),
        leading,
    )


def on_device(site_tensors, left_edge, right_edge, order, bitstrings):
    col_count = lax.axis_size("col")
    col_index = lax.axis_index("col")
    tensors = site_tensors[0].astype(jnp.float32)
    site_bits = jnp.take(bitstrings, order, axis=1)
    batch_rows = site_bits.shape[0]
    bond_size = left_edge.shape[1]
    product = column_product(tensors, site_bits)
    share = (batch_rows + col_count - 1) // col_count
    padded_rows = share * col_count
    grouped = product.reshape(col_count, share, bond_size, 2 * bond_size)
    received = lax.all_to_all(grouped, "col", split_axis=0, concat_axis=0, tiled=True)
    items = received.shape[1]
    start = jnp.broadcast_to(left_edge[0], (items, bond_size, 2 * bond_size))
    final_state = lax.fori_loop(
        0,
        received.shape[0],
        lambda position, carried: complex_product(
            carried, lax.dynamic_index_in_dim(received, position, 0, keepdims=False)
        ),
        start,
    )
    closed = closing(final_state, right_edge[0])
    placed = lax.dynamic_update_slice(
        jnp.zeros((2, padded_rows), jnp.float32), closed, (jnp.int32(0), col_index * share)
    )
    return lax.psum(placed, ("col", "slc"))


def solution(mesh):
    return jax.shard_map(
        on_device,
        mesh=mesh,
        in_specs=(
            P(("grp", "slc"), "col", None, None, None),
            P(("grp", "slc"), None, None),
            P(("grp", "slc"), None, None),
            P(("grp", "col")),
            P(("grp", "bat"), None),
        ),
        out_specs=P(None, ("grp", "bat")),
        check_vma=False,
    )
```

profile of v0, /device:TPU:0, one launch (start us, length us, event | category | flops | bytes accessed | tf_op | source)
XLA Modules:
  0.0 143.9 jit_solution(12536998118196753343)
XLA Ops:
  4.4 83.2 %while.28 = (s32[]{:T(128)}, f32[32,64,128]{2,1,0:T(8,128)}, s32[32,18]{0,1:T(8,128)S(1)}, f32[18,2,64,128]{3,2,1,0:T(8,128)S(1)}, s32[]{:T(128)}, /*index=5*/s32[]{:T(128)}, s32[]{:T(128)}, s32[]{}) while((s32[]{:T(128)}, f32[32,64,128]{2,1,0:T(8,128)}, s32[32,18]{0,1:T(8,128)S(1)}, f32[18,2,64,128]{3,2,1,0:T(8,128)S(1)}, s32[]{:T(128)}, ...), condition=%wide.region_1.2_spmd, body=%wide.region_0.1_spmd.sunk | while | flops 404095008 | bytes 9634135 | solution.py:37
  4.9 1.2 copy.22
  6.2 3.1 %fusion.26 = f32[32,64,128]{2,1,0:T(8,128)} fusion(f32[32,64,128]{2,1,0:T(8,128)S(1)} %copy.22, f32[32,64,64]{2,1,0:T(8,128)S(1)} %get-tuple-element.256, f32[32,64,64]{2,1,0:T(8,128)S(1)} %get-tuple-element.257, f32[32,64,128]{2,1,0:T(8,128)S(1)} %broadcast_select_fusion.3), kind=kOutput, calls=%fused_computation.7.clone.1 | convolution fusion | flops 403701760 | bytes 4194304 | tf_op jit(solution)/shard_map/while/body/eval_jaxpr/bij,bjk->bik/dot_general | solution.py:14
  9.8 1.2 copy.22
  11.1 3.1 %fusion.26 = f32[32,64,128]{2,1,0:T(8,128)} fusion(f32[32,64,128]{2,1,0:T(8,128)S(1)} %copy.22, f32[32,64,64]{2,1,0:T(8,128)S(1)} %get-tuple-element.256, f32[32,64,64]{2,1,0:T(8,128)S(1)} %get-tuple-element.257, f32[32,64,128]{2,1,0:T(8,128)S(1)} %broadcast_select_fusion.3), kind=kOutput, calls=%fused_computation.7.clone.1 | convolution fusion | flops 403701760 | bytes 4194304 | tf_op jit(solution)/shard_map/while/body/eval_jaxpr/bij,bjk->bik/dot_general | solution.py:14
  14.7 1.2 copy.22
  16.0 3.1 %fusion.26 = f32[32,64,128]{2,1,0:T(8,128)} fusion(f32[32,64,128]{2,1,0:T(8,128)S(1)} %copy.22, f32[32,64,64]{2,1,0:T(8,128)S(1)} %get-tuple-element.256, f32[32,64,64]{2,1,0:T(8,128)S(1)} %get-tuple-element.257, f32[32,64,128]{2,1,0:T(8,128)S(1)} %broadcast_select_fusion.3), kind=kOutput, calls=%fused_computation.7.clone.1 | convolution fusion | flops 403701760 | bytes 4194304 | tf_op jit(solution)/shard_map/while/body/eval_jaxpr/bij,bjk->bik/dot_general | solution.py:14
  19.6 1.2 copy.22
  20.9 3.1 %fusion.26 = f32[32,64,128]{2,1,0:T(8,128)} fusion(f32[32,64,128]{2,1,0:T(8,128)S(1)} %copy.22, f32[32,64,64]{2,1,0:T(8,128)S(1)} %get-tuple-element.256, f32[32,64,64]{2,1,0:T(8,128)S(1)} %get-tuple-element.257, f32[32,64,128]{2,1,0:T(8,128)S(1)} %broadcast_select_fusion.3), kind=kOutput, calls=%fused_computation.7.clone.1 | convolution fusion | flops 403701760 | bytes 4194304 | tf_op jit(solution)/shard_map/while/body/eval_jaxpr/bij,bjk->bik/dot_general | solution.py:14
  24.5 1.2 copy.22
  25.8 3.1 %fusion.26 = f32[32,64,128]{2,1,0:T(8,128)} fusion(f32[32,64,128]{2,1,0:T(8,128)S(1)} %copy.22, f32[32,64,64]{2,1,0:T(8,128)S(1)} %get-tuple-element.256, f32[32,64,64]{2,1,0:T(8,128)S(1)} %get-tuple-element.257, f32[32,64,128]{2,1,0:T(8,128)S(1)} %broadcast_select_fusion.3), kind=kOutput, calls=%fused_computation.7.clone.1 | convolution fusion | flops 403701760 | bytes 4194304 | tf_op jit(solution)/shard_map/while/body/eval_jaxpr/bij,bjk->bik/dot_general | solution.py:14
  29.4 1.2 copy.22
  30.7 3.1 %fusion.26 = f32[32,64,128]{2,1,0:T(8,128)} fusion(f32[32,64,128]{2,1,0:T(8,128)S(1)} %copy.22, f32[32,64,64]{2,1,0:T(8,128)S(1)} %get-tuple-element.256, f32[32,64,64]{2,1,0:T(8,128)S(1)} %get-tuple-element.257, f32[32,64,128]{2,1,0:T(8,128)S(1)} %broadcast_select_fusion.3), kind=kOutput, calls=%fused_computation.7.clone.1 | convolution fusion | flops 403701760 | bytes 4194304 | tf_op jit(solution)/shard_map/while/body/eval_jaxpr/bij,bjk->bik/dot_general | solution.py:14
  34.3 1.2 copy.22
  35.5 3.1 %fusion.26 = f32[32,64,128]{2,1,0:T(8,128)} fusion(f32[32,64,128]{2,1,0:T(8,128)S(1)} %copy.22, f32[32,64,64]{2,1,0:T(8,128)S(1)} %get-tuple-element.256, f32[32,64,64]{2,1,0:T(8,128)S(1)} %get-tuple-element.257, f32[32,64,128]{2,1,0:T(8,128)S(1)} %broadcast_select_fusion.3), kind=kOutput, calls=%fused_computation.7.clone.1 | convolution fusion | flops 403701760 | bytes 4194304 | tf_op jit(solution)/shard_map/while/body/eval_jaxpr/bij,bjk->bik/dot_general | solution.py:14
  39.2 1.2 copy.22
  40.4 3.1 %fusion.26 = f32[32,64,128]{2,1,0:T(8,128)} fusion(f32[32,64,128]{2,1,0:T(8,128)S(1)} %copy.22, f32[32,64,64]{2,1,0:T(8,128)S(1)} %get-tuple-element.256, f32[32,64,64]{2,1,0:T(8,128)S(1)} %get-tuple-element.257, f32[32,64,128]{2,1,0:T(8,128)S(1)} %broadcast_select_fusion.3), kind=kOutput, calls=%fused_computation.7.clone.1 | convolution fusion | flops 403701760 | bytes 4194304 | tf_op jit(solution)/shard_map/while/body/eval_jaxpr/bij,bjk->bik/dot_general | solution.py:14
  44.1 1.2 copy.22
  45.3 3.1 %fusion.26 = f32[32,64,128]{2,1,0:T(8,128)} fusion(f32[32,64,128]{2,1,0:T(8,128)S(1)} %copy.22, f32[32,64,64]{2,1,0:T(8,128)S(1)} %get-tuple-element.256, f32[32,64,64]{2,1,0:T(8,128)S(1)} %get-tuple-element.257, f32[32,64,128]{2,1,0:T(8,128)S(1)} %broadcast_select_fusion.3), kind=kOutput, calls=%fused_computation.7.clone.1 | convolution fusion | flops 403701760 | bytes 4194304 | tf_op jit(solution)/shard_map/while/body/eval_jaxpr/bij,bjk->bik/dot_general | solution.py:14
  49.0 1.2 copy.22
  50.2 3.1 %fusion.26 = f32[32,64,128]{2,1,0:T(8,128)} fusion(f32[32,64,128]{2,1,0:T(8,128)S(1)} %copy.22, f32[32,64,64]{2,1,0:T(8,128)S(1)} %get-tuple-element.256, f32[32,64,64]{2,1,0:T(8,128)S(1)} %get-tuple-element.257, f32[32,64,128]{2,1,0:T(8,128)S(1)} %broadcast_select_fusion.3), kind=kOutput, calls=%fused_computation.7.clone.1 | convolution fusion | flops 403701760 | bytes 4194304 | tf_op jit(solution)/shard_map/while/body/eval_jaxpr/bij,bjk->bik/dot_general | solution.py:14
  55.1 3.1 %fusion.26 = f32[32,64,128]{2,1,0:T(8,128)} fusion(f32[32,64,128]{2,1,0:T(8,128)S(1)} %copy.22, f32[32,64,64]{2,1,0:T(8,128)S(1)} %get-tuple-element.256, f32[32,64,64]{2,1,0:T(8,128)S(1)} %get-tuple-element.257, f32[32,64,128]{2,1,0:T(8,128)S(1)} %broadcast_select_fusion.3), kind=kOutput, calls=%fused_computation.7.clone.1 | convolution fusion | flops 403701760 | bytes 4194304 | tf_op jit(solution)/shard_map/while/body/eval_jaxpr/bij,bjk->bik/dot_general | solution.py:14
  60.0 3.1 %fusion.26 = f32[32,64,128]{2,1,0:T(8,128)} fusion(f32[32,64,128]{2,1,0:T(8,128)S(1)} %copy.22, f32[32,64,64]{2,1,0:T(8,128)S(1)} %get-tuple-element.256, f32[32,64,64]{2,1,0:T(8,128)S(1)} %get-tuple-element.257, f32[32,64,128]{2,1,0:T(8,128)S(1)} %broadcast_select_fusion.3), kind=kOutput, calls=%fused_computation.7.clone.1 | convolution fusion | flops 403701760 | bytes 4194304 | tf_op jit(solution)/shard_map/while/body/eval_jaxpr/bij,bjk->bik/dot_general | solution.py:14
  64.9 3.1 %fusion.26 = f32[32,64,128]{2,1,0:T(8,128)} fusion(f32[32,64,128]{2,1,0:T(8,128)S(1)} %copy.22, f32[32,64,64]{2,1,0:T(8,128)S(1)} %get-tuple-element.256, f32[32,64,64]{2,1,0:T(8,128)S(1)} %get-tuple-element.257, f32[32,64,128]{2,1,0:T(8,128)S(1)} %broadcast_select_fusion.3), kind=kOutput, calls=%fused_computation.7.clone.1 | convolution fusion | flops 403701760 | bytes 4194304 | tf_op jit(solution)/shard_map/while/body/eval_jaxpr/bij,bjk->bik/dot_general | solution.py:14
  69.8 3.1 %fusion.26 = f32[32,64,128]{2,1,0:T(8,128)} fusion(f32[32,64,128]{2,1,0:T(8,128)S(1)} %copy.22, f32[32,64,64]{2,1,0:T(8,128)S(1)} %get-tuple-element.256, f32[32,64,64]{2,1,0:T(8,128)S(1)} %get-tuple-element.257, f32[32,64,128]{2,1,0:T(8,128)S(1)} %broadcast_select_fusion.3), kind=kOutput, calls=%fused_computation.7.clone.1 | convolution fusion | flops 403701760 | bytes 4194304 | tf_op jit(solution)/shard_map/while/body/eval_jaxpr/bij,bjk->bik/dot_general | solution.py:14
  74.7 3.1 %fusion.26 = f32[32,64,128]{2,1,0:T(8,128)} fusion(f32[32,64,128]{2,1,0:T(8,128)S(1)} %copy.22, f32[32,64,64]{2,1,0:T(8,128)S(1)} %get-tuple-element.256, f32[32,64,64]{2,1,0:T(8,128)S(1)} %get-tuple-element.257, f32[32,64,128]{2,1,0:T(8,128)S(1)} %broadcast_select_fusion.3), kind=kOutput, calls=%fused_computation.7.clone.1 | convolution fusion | flops 403701760 | bytes 4194304 | tf_op jit(solution)/shard_map/while/body/eval_jaxpr/bij,bjk->bik/dot_general | solution.py:14
  79.6 3.1 %fusion.26 = f32[32,64,128]{2,1,0:T(8,128)} fusion(f32[32,64,128]{2,1,0:T(8,128)S(1)} %copy.22, f32[32,64,64]{2,1,0:T(8,128)S(1)} %get-tuple-element.256, f32[32,64,64]{2,1,0:T(8,128)S(1)} %get-tuple-element.257, f32[32,64,128]{2,1,0:T(8,128)S(1)} %broadcast_select_fusion.3), kind=kOutput, calls=%fused_computation.7.clone.1 | convolution fusion | flops 403701760 | bytes 4194304 | tf_op jit(solution)/shard_map/while/body/eval_jaxpr/bij,bjk->bik/dot_general | solution.py:14
  84.5 3.1 %fusion.26 = f32[32,64,128]{2,1,0:T(8,128)} fusion(f32[32,64,128]{2,1,0:T(8,128)S(1)} %copy.22, f32[32,64,64]{2,1,0:T(8,128)S(1)} %get-tuple-element.256, f32[32,64,64]{2,1,0:T(8,128)S(1)} %get-tuple-element.257, f32[32,64,128]{2,1,0:T(8,128)S(1)} %broadcast_select_fusion.3), kind=kOutput, calls=%fused_computation.7.clone.1 | convolution fusion | flops 403701760 | bytes 4194304 | tf_op jit(solution)/shard_map/while/body/eval_jaxpr/bij,bjk->bik/dot_general | solution.py:14
  87.6 6.5 %all-to-all-start = ((f32[4,8,64,128]{3,2,1,0:T(8,128)}), f32[4,8,64,128]{3,2,1,0:T(8,128)S(1)}, u32[]{:S(2)}, u32[]{:S(2)}) async-start(f32[4,8,64,128]{3,2,1,0:T(8,128)} %bitcast.13), calls=%async_computation | async-start | bytes 2097152 | tf_op jit(solution)/shard_map/all_to_all | solution.py:58
  94.2 25.6 %all-to-all-done = f32[4,8,64,128]{3,2,1,0:T(8,128)S(1)} async-done(((f32[4,8,64,128]{3,2,1,0:T(8,128)}), f32[4,8,64,128]{3,2,1,0:T(8,128)S(1)}, u32[]{:S(2)}, u32[]{:S(2)}) %all-to-all-start) | async-done | bytes 1048608 | tf_op jit(solution)/shard_map/all_to_all | solution.py:58
  119.8 3.4 %while.29 = (s32[]{:T(128)}, f32[8,64,128]{2,1,0:T(8,128)S(1)}, f32[4,8,64,128]{3,2,1,0:T(8,128)S(1)}, s32[]{:T(128)}) while((s32[]{:T(128)}, f32[8,64,128]{2,1,0:T(8,128)S(1)}, f32[4,8,64,128]{3,2,1,0:T(8,128)S(1)}, s32[]{:T(128)}) %tuple.74), condition=%wide.region_3.4_spmd, body=%wide.region_2.3_spmd.sunk | while | flops 100958208 | bytes 2621497 | solution.py:61
  123.7 20.2 %psum.7 = f32[2,32]{1,0:T(2,128)} all-reduce(f32[2,32]{1,0:T(2,128)S(1)} %dynamic_update_slice.3), channel_id=1, replica_groups=mesh['grp'=2,'col'=4,'slc'=2,'bat'=2] {'col','slc'}, use_global_device_ids=true, to_apply=%region_6.7 | all-reduce | flops 64 | bytes 512 | tf_op jit(solution)/shard_map/psum | solution.py:73
  (113 shorter events, 25.8 us)
Async XLA Ops:
  0.0 2.5 %copy-start.2 = (s32[32,72]{1,0:T(8,128)S(1)}, s32[32,72]{1,0:T(8,128)}, u32[]{:S(2)}) copy-start(s32[32,72]{1,0:T(8,128)} %param.13) | copy-start | bytes 27652
  87.6 6.5 %copy-start = (f32[1,64,128]{2,1,0:T(8,128)S(1)}, f32[1,64,128]{2,1,0:T(8,128)}, u32[]{:S(2)}) copy-start(f32[1,64,128]{2,1,0:T(8,128)} %param.11) | copy-start | bytes 98308
  87.6 32.2 %copy-start.1 = (f32[1,64,128]{2,1,0:T(8,128)S(1)}, f32[1,64,128]{2,1,0:T(8,128)}, u32[]{:S(2)}) copy-start(f32[1,64,128]{2,1,0:T(8,128)} %param.10) | copy-start | bytes 98308
  87.6 32.2 %all-to-all-start = ((f32[4,8,64,128]{3,2,1,0:T(8,128)}), f32[4,8,64,128]{3,2,1,0:T(8,128)S(1)}, u32[]{:S(2)}, u32[]{:S(2)}) async-start(f32[4,8,64,128]{3,2,1,0:T(8,128)} %bitcast.13), calls=%async_computation | async-start | bytes 2097152 | tf_op jit(solution)/shard_map/all_to_all | solution.py:58
where the time goes:
time: 145 us; the launch traced here: 144 us
  matrix products  55.4 us (38%)
  waiting for transfers between devices  25.6 us (18%)
  local copies, waits for them, and re-layouts  22.1 us (15%)
  blocking collectives  20.2 us (14%)
  other arithmetic  13.5 us (9%)
  starting transfers between devices  6.48 us (4%)
    dot_general x21, matrix products, complex_product(): jnp.einsum('bij,bjk->bik', first_factor, stacked, precision=lax.Precision...  55.4 us
    all_to_all x1, waiting for transfers between devices, on_device(): lax.all_to_all(grouped, 'col', split_axis=0, concat_axis=0, tiled=True)  25.6 us
    while x21, local copies, waits for them, and re-layouts  21 us
    psum x1, blocking collectives, on_device(): return lax.psum(placed, ('col', 'slc'))  20.2 us
    neg x21, other arithmetic, rotate(): return jnp.concatenate([-block[..., middle:], block[..., :middle]], axis=-1)  7.05 us
    all_to_all x1, starting transfers between devices, on_device(): lax.all_to_all(grouped, 'col', split_axis=0, concat_axis=0, tiled=True)  6.48 us
    select_n x18, other arithmetic, select_site(): return jnp.where(chosen_bits[:, None, None] == 1, matrices[1], matrices[0])  3.41 us
  transfers between devices with their start and end apart: 1, of which 1 were waited for; matrix products, arithmetic and copies ran while one was open for 0% of the time, Pallas kernels for 0%

commit v1 on v0

v1 whole, which is shorter than its diff:
```python
import functools

import jax
import jax.numpy as jnp
from jax import lax
from jax.experimental import pallas as pl
from jax.experimental.pallas import tpu as pltpu
from jax.sharding import PartitionSpec as P

MESH = pl.DeviceIdType.MESH
GROUPS = 4
PIECES = 2
UNROLL = 2


def split(x):
    high = x.astype(jnp.bfloat16)
    low = (x - high.astype(jnp.float32)).astype(jnp.bfloat16)
    return high, low


def rotate(block):
    lanes = lax.broadcasted_iota(jnp.int32, block.shape, block.ndim - 1)
    middle = block.shape[-1] // 2
    rolled = pltpu.roll(block, middle, block.ndim - 1)
    return jnp.where(lanes < middle, -rolled, rolled)


def complex_product(first, second):
    first_high, first_low = split(first)
    high, low = split(second)
    turned_high, turned_low = split(rotate(second))
    left = jnp.concatenate([first_high, first_low], axis=0)
    right = jnp.concatenate(
        [
            jnp.concatenate([high, low], axis=1),
            jnp.concatenate([turned_high, turned_low], axis=1),
        ],
        axis=0,
    )
    out = jnp.dot(left, right, preferred_element_type=jnp.float32)
    chi = first.shape[0]
    wide = first.shape[1]
    small = out[:chi, wide:] + out[chi:, :wide] + out[chi:, wide:]
    return out[:chi, :wide] + small


def kernel(
    n_col,
    n_slc,
    groups,
    pieces,
    order_ref,
    bits_ref,
    tensors_ref,
    left_ref,
    right_ref,
    out_ref,
    weights,
    state,
    start,
    mine,
    arrived,
    closing_rows,
    share,
    finals,
    send_right,
    recv_right,
    send_left,
    recv_left,
    send_final,
    recv_final,
):
    col = lax.axis_index("col")
    slc = lax.axis_index("slc")
    sites = tensors_ref.shape[1]
    chi, wide = tensors_ref.shape[3], tensors_ref.shape[4]
    batch = bits_ref.shape[0]
    half = batch // 2
    per = half // groups
    chunk = per // pieces
    peers = n_col * n_slc
    me = col * n_slc + slc
    last = n_col - 1

    barrier = pltpu.get_barrier_semaphore()

    def greet(peer, carry):
        @pl.when(peer != me)
        def _():
            pl.semaphore_signal(
                barrier,
                inc=1,
                device_id={"col": peer // n_slc, "slc": lax.rem(peer, n_slc)},
                device_id_type=MESH,
            )

        return carry

    lax.fori_loop(0, peers, greet, 0)

    def build(site, carry):
        for bit in range(2):
            matrix = tensors_ref[0, site, bit].astype(jnp.float32)
            turned = rotate(matrix).astype(jnp.bfloat16)
            plain = matrix.astype(jnp.bfloat16)
            lanes = pl.ds(bit * wide, wide)
            for copy in range(2):
                weights[site, pl.ds(copy * wide, chi), lanes] = plain
                weights[site, pl.ds(copy * wide + chi, chi), lanes] = turned
        return carry

    lax.fori_loop(0, sites, build, 0)

    rows = lax.broadcasted_iota(jnp.int32, (chi, wide), 0)
    lanes = lax.broadcasted_iota(jnp.int32, (chi, wide), 1)
    unit = (rows == lanes).astype(jnp.float32)
    is_first = jnp.broadcast_to(col, (chi, wide)) == 0
    begin = jnp.where(is_first, left_ref[0], unit)
    begin_high, begin_low = split(begin)
    start[:, :wide] = begin_high
    start[:, wide:] = begin_low
    closing_rows[...] = jnp.zeros_like(closing_rows)

    def right_copy(piece):
        where = pl.ds(piece * chunk, chunk)
        return pltpu.make_async_remote_copy(
            src_ref=mine.at[where],
            dst_ref=arrived.at[where],
            send_sem=send_right.at[piece],
            recv_sem=recv_right.at[piece],
            device_id={"col": lax.rem(col + 1, n_col)},
            device_id_type=MESH,
        )

    def left_copy(piece):
        where = pl.ds(half + piece * chunk, chunk)
        return pltpu.make_async_remote_copy(
            src_ref=mine.at[where],
            dst_ref=arrived.at[where],
            send_sem=send_left.at[piece],
            recv_sem=recv_left.at[piece],
            device_id={"col": lax.rem(col + last, n_col)},
            device_id_type=MESH,
        )

    def item_of(group, at):
        base = 0 if at < per else half - per
        return base + group * per + at

    def advance(site, group, final):
        qubit = order_ref[site]
        block = weights[site]
        for at in range(2 * per):
            where = pl.ds(at * chi, chi)
            both = jnp.dot(state[where, :], block, preferred_element_type=jnp.float32)
            item = item_of(group, at)
            bit = jnp.broadcast_to(bits_ref[item, qubit], (chi, wide))
            chosen = jnp.where(bit == 1, both[:, wide:], both[:, :wide])
            if final:
                mine[item] = chosen
            else:
                high, low = split(chosen)
                state[where, :wide] = high
                state[where, wide:] = low

    def column(group):
        for at in range(2 * per):
            state[pl.ds(at * chi, chi), :] = start[...]

        def step(site, carry):
            advance(site, group, False)
            return carry

        lax.fori_loop(0, sites - 1, step, 0, unroll=UNROLL)
        advance(sites - 1, group, True)

    def close(item, row, value):
        edge = right_ref[0]
        turned = rotate(edge)
        signed = jnp.where(lanes < chi, edge, -edge)
        crossed = jnp.where(lanes < chi, -turned, turned)
        real_row = jnp.sum(value * signed, axis=0, keepdims=True)
        imag_row = jnp.sum(value * crossed, axis=0, keepdims=True)
        closing_rows[pl.ds(row, 1), :] = real_row
        closing_rows[pl.ds(half + row, 1), :] = imag_row

    def merge_right(group):
        for piece_at in range(pieces):
            piece = group * pieces + piece_at
            right_copy(piece).wait_recv()
            for at in range(chunk):
                item = piece * chunk + at
                mine[item] = complex_product(arrived[item], mine[item])

            @pl.when(col < last)
            def _():
                right_copy(piece).start()

            @pl.when(col == last)
            def _():
                for at in range(chunk):
                    item = piece * chunk + at
                    close(item, item, mine[item])

    def merge_left(group):
        for piece_at in range(pieces):
            piece = group * pieces + piece_at
            left_copy(piece).wait_recv()
            for at in range(chunk):
                item = half + piece * chunk + at
                mine[item] = complex_product(mine[item], arrived[item])

            @pl.when(col > 0)
            def _():
                left_copy(piece).start()

            @pl.when(col == 0)
            def _():
                for at in range(chunk):
                    item = half + piece * chunk + at
                    close(item, piece * chunk + at, mine[item])

    def slot(turn, carry):
        @pl.when(turn < groups)
        def _():
            column(turn)

            @pl.when(turn == 0)
            def _():
                pl.semaphore_wait(barrier, peers - 1)

            @pl.when(col == 0)
            def _():
                for at in range(pieces):
                    right_copy(turn * pieces + at).start()

            @pl.when(col == last)
            def _():
                for at in range(pieces):
                    left_copy(turn * pieces + at).start()

        from_left = turn - col

        @pl.when((col > 0) & (from_left >= 0) & (from_left < groups))
        def _():
            merge_right(from_left)

        from_right = turn - (last - col)

        @pl.when((col < last) & (from_right >= 0) & (from_right < groups))
        def _():
            merge_left(from_right)

        return carry

    lax.fori_loop(0, groups + last, slot, 0)

    def final_copy(peer, place):
        return pltpu.make_async_remote_copy(
            src_ref=share,
            dst_ref=finals.at[place],
            send_sem=send_final.at[peer],
            recv_sem=recv_final.at[place],
            device_id={"col": peer // n_slc, "slc": lax.rem(peer, n_slc)},
            device_id_type=MESH,
        )

    closer = (col == 0) | (col == last)
    place = jnp.where(col == last, slc, n_slc + slc)

    @pl.when(closer)
    def _():
        totals = jnp.sum(closing_rows[...].T, axis=0, keepdims=True)
        tile = jnp.broadcast_to(totals, share.shape)
        share[...] = tile
        finals[place] = tile

        def send(peer, carry):
            @pl.when(peer != me)
            def _():
                final_copy(peer, place).start()

            return carry

        lax.fori_loop(0, peers, send, 0)

    for side in range(2):
        for part in range(n_slc):
            source_col = last if side == 0 else 0

            @pl.when((col != source_col) | (slc != part))
            def _():
                final_copy(me, side * n_slc + part).wait_recv()

    sums = []
    for side in range(2):
        total = finals[side * n_slc]
        for part in range(1, n_slc):
            total = total + finals[side * n_slc + part]
        sums.append(total)
    ahead, behind = sums
    columns = lax.broadcasted_iota(jnp.int32, share.shape, 1)
    width = share.shape[1]
    real = jnp.where(columns < half, ahead, pltpu.roll(behind, half, 1))
    imag = jnp.where(columns < half, pltpu.roll(ahead, width - half, 1), behind)
    out_ref[0:1, :] = real[0:1, :batch]
    out_ref[1:2, :] = imag[0:1, :batch]

    @pl.when(closer)
    def _():
        def done(peer, carry):
            @pl.when(peer != me)
            def _():
                final_copy(peer, place).wait_send()

            return carry

        lax.fori_loop(0, peers, done, 0)

    @pl.when(col < last)
    def _():
        for piece in range(groups * pieces):
            right_copy(piece).wait_send()

    @pl.when(col > 0)
    def _():
        for piece in range(groups * pieces):
            left_copy(piece).wait_send()


def on_device(site_tensors, left_edge, right_edge, order, bitstrings):
    n_col = lax.axis_size("col")
    n_slc = lax.axis_size("slc")
    batch = bitstrings.shape[0]
    half = batch // 2
    groups = GROUPS
    pieces = PIECES
    sites, chi, wide = site_tensors.shape[1], site_tensors.shape[3], site_tensors.shape[4]
    peers = n_col * n_slc
    chunks = groups * pieces
    vmem = pl.BlockSpec(memory_space=pltpu.VMEM)
    smem = pl.BlockSpec(memory_space=pltpu.SMEM)
    lane_rows = 128
    return pl.pallas_call(
        functools.partial(kernel, n_col, n_slc, groups, pieces),
        out_shape=jax.ShapeDtypeStruct((2, batch), jnp.float32),
        in_specs=[smem, smem, vmem, vmem, vmem],
        out_specs=vmem,
        scratch_shapes=[
            pltpu.VMEM((sites, 2 * wide, 2 * wide), jnp.bfloat16),
            pltpu.VMEM((batch // groups * chi, 2 * wide), jnp.bfloat16),
            pltpu.VMEM((chi, 2 * wide), jnp.bfloat16),
            pltpu.VMEM((batch, chi, wide), jnp.float32),
            pltpu.VMEM((batch, chi, wide), jnp.float32),
            pltpu.VMEM((lane_rows, wide), jnp.float32),
            pltpu.VMEM((8, lane_rows), jnp.float32),
            pltpu.VMEM((2 * n_slc, 8, lane_rows), jnp.float32),
            pltpu.SemaphoreType.DMA((chunks,)),
            pltpu.SemaphoreType.DMA((chunks,)),
            pltpu.SemaphoreType.DMA((chunks,)),
            pltpu.SemaphoreType.DMA((chunks,)),
            pltpu.SemaphoreType.DMA((peers,)),
            pltpu.SemaphoreType.DMA((2 * n_slc,)),
        ],
        compiler_params=pltpu.CompilerParams(collective_id=0, has_side_effects=True),
    )(order, bitstrings, site_tensors, left_edge, right_edge)


def solution(mesh):
    return jax.shard_map(
        on_device,
        mesh=mesh,
        in_specs=(
            P(("grp", "slc"), "col", None, None, None),
            P(("grp", "slc"), None, None),
            P(("grp", "slc"), None, None),
            P(("grp", "col")),
            P(("grp", "bat"), None),
        ),
        out_specs=P(None, ("grp", "bat")),
        check_vma=False,
    )
```

time: 145 us -> 44.5 us (0.31)
  matrix products: 55.4 us -> 0 us
  Pallas kernels: 0 us -> 43.1 us
  waiting for transfers between devices: 25.6 us -> 0 us
  local copies, waits for them, and re-layouts: 22.1 us -> 1.24 us
  blocking collectives: 20.2 us -> 0 us
  other arithmetic: 13.5 us -> 0 us
  starting transfers between devices: 6.48 us -> 0 us
    dot_general x21 -> x0, matrix products: 55.4 us -> none  [complex_product(): jnp.einsum('bij,bjk->bik', first_factor, stacked, precision=lax.Precision...]
    pallas_call x0 -> x1, Pallas kernels: none -> 43.1 us  [on_device(): pl.pallas_call(functools.partial(kernel, n_col, n_slc, groups, pieces), o...]
    all_to_all x1 -> x0, waiting for transfers between devices: 25.6 us -> none  [on_device(): lax.all_to_all(grouped, 'col', split_axis=0, concat_axis=0, tiled=True)]
    while x21 -> x0, local copies, waits for them, and re-layouts: 21 us -> none
    psum x1 -> x0, blocking collectives: 20.2 us -> none  [on_device(): return lax.psum(placed, ('col', 'slc'))]
    neg x21 -> x0, other arithmetic: 7.05 us -> none  [rotate(): return jnp.concatenate([-block[..., middle:], block[..., :middle]], axis=-1)]
    all_to_all x1 -> x0, starting transfers between devices: 6.48 us -> none  [on_device(): lax.all_to_all(grouped, 'col', split_axis=0, concat_axis=0, tiled=True)]
    select_n x20 -> x0, other arithmetic: 4.15 us -> none  [the longest x18 3.41 us: select_site(): return jnp.where(chosen_bits[:, None, None] == 1, matrices[1], matrices[0])]
  transfers between devices with their start and end apart: 1 -> 0, of which waited for: 1 -> 0; matrix products, arithmetic and copies ran while one was open for 0% -> 0% of each run, Pallas kernels for 0% -> 0%
where the time goes in v1:
time: 44.5 us; the launch traced here: 44.4 us
  Pallas kernels  43.1 us (97%)
  local copies, waits for them, and re-layouts  1.24 us (3%)
    pallas_call x1, Pallas kernels, on_device(): pl.pallas_call(functools.partial(kernel, n_col, n_slc, groups, pieces), o...  43.1 us
    unnamed x1, local copies, waits for them, and re-layouts  1.24 us

profile of v1, /device:TPU:0, one launch (start us, length us, event | category | flops | bytes accessed | tf_op | source)
XLA Modules:
  0.0 44.4 jit_solution(4290602453492040007)
XLA Ops:
  0.0 43.1 %shard_map.55 = f32[2,32]{1,0:T(2,128)} custom-call(s32[18]{0:T(128)} %order_ref.1, s32[32,72]{1,0:T(8,128)} %bits_ref.1, bf16[1,18,2,64,128]{4,3,2,1,0:T(8,128)(2,1)} %tensors_ref.1, f32[1,64,128]{2,1,0:T(8,128)} %left_ref.1, f32[1,64,128]{2,1,0:T(8,128)} %right_ref.1), custom_call_target="tpu_custom_call" | custom-call | tf_op jit(solution)/shard_map/pallas_call | solution.py:345
  43.1 1.2 %copy.7 = f32[2,32]{1,0:T(2,128)} copy(f32[2,32]{1,0:T(2,128)} %shard_map.55) | data formatting | bytes 512

commit v2 on v1

--- a/solution.py
+++ b/solution.py
@@ -8,9 +8,10 @@
 from jax.sharding import PartitionSpec as P
 
 MESH = pl.DeviceIdType.MESH
-GROUPS = 4
-PIECES = 2
-UNROLL = 2
+GROUPS = 8
+PIECES = 1
+LAG = 2
+DEPTH = 5
 
 
 def split(x):
@@ -26,23 +27,52 @@
     return jnp.where(lanes < middle, -rolled, rolled)
 
 
-def complex_product(first, second):
-    first_high, first_low = split(first)
-    high, low = split(second)
-    turned_high, turned_low = split(rotate(second))
-    left = jnp.concatenate([first_high, first_low], axis=0)
-    right = jnp.concatenate(
+def left_form(x):
+    high, low = split(x)
+    return jnp.concatenate([high, low], axis=0)
+
+
+def right_form(x):
+    high, low = split(x)
+    turned_high, turned_low = split(rotate(x))
+    return jnp.concatenate(
         [
             jnp.concatenate([high, low], axis=1),
             jnp.concatenate([turned_high, turned_low], axis=1),
         ],
         axis=0,
     )
+
+
+def form_product(left, right):
     out = jnp.dot(left, right, preferred_element_type=jnp.float32)
-    chi = first.shape[0]
-    wide = first.shape[1]
+    chi = left.shape[0] // 2
+    wide = left.shape[1]
     small = out[:chi, wide:] + out[chi:, :wide] + out[chi:, wide:]
     return out[:chi, :wide] + small
+
+
+def complex_product(first, second):
+    return form_product(left_form(first), right_form(second))
+
+
+def segments_of(sites):
+    count = -(-sites // DEPTH)
+    sizes = [sites // count + (1 if at < sites % count else 0) for at in range(count)]
+    starts = [sum(sizes[:at]) for at in range(count)]
+    return list(zip(starts, sizes))
+
+
+def site_weights(first, second):
+    plain = jnp.concatenate([first, second], axis=1)
+    turned = jnp.concatenate(
+        [
+            rotate(first.astype(jnp.float32)).astype(jnp.bfloat16),
+            rotate(second.astype(jnp.float32)).astype(jnp.bfloat16),
+        ],
+        axis=1,
+    )
+    return jnp.concatenate([plain, turned, plain, turned], axis=0)
 
 
 def kernel(
@@ -56,9 +86,9 @@
     left_ref,
     right_ref,
     out_ref,
-    weights,
     state,
-    start,
+    first_table,
+    other_table,
     mine,
     arrived,
     closing_rows,
@@ -99,27 +129,48 @@
 
     lax.fori_loop(0, peers, greet, 0)
 
-    def build(site, carry):
-        for bit in range(2):
-            matrix = tensors_ref[0, site, bit].astype(jnp.float32)
-            turned = rotate(matrix).astype(jnp.bfloat16)
-            plain = matrix.astype(jnp.bfloat16)
-            lanes = pl.ds(bit * wide, wide)
-            for copy in range(2):
-                weights[site, pl.ds(copy * wide, chi), lanes] = plain
-                weights[site, pl.ds(copy * wide + chi, chi), lanes] = turned
-        return carry
-
-    lax.fori_loop(0, sites, build, 0)
-
     rows = lax.broadcasted_iota(jnp.int32, (chi, wide), 0)
     lanes = lax.broadcasted_iota(jnp.int32, (chi, wide), 1)
     unit = (rows == lanes).astype(jnp.float32)
     is_first = jnp.broadcast_to(col, (chi, wide)) == 0
     begin = jnp.where(is_first, left_ref[0], unit)
-    begin_high, begin_low = split(begin)
-    start[:, :wide] = begin_high
-    start[:, wide:] = begin_low
+    segments = segments_of(sites)
+    bases = []
+    entries = 0
+    for at, (_, size) in enumerate(segments):
+        bases.append(entries)
+        entries += 0 if at == 0 else 2**size
+
+    def put(segment, size, level, entry, value):
+        if level < size:
+            high, low = split(value)
+            where = pl.ds(entry * chi, chi)
+            state[segment, where, :wide] = high
+            state[segment, where, wide:] = low
+        elif segment == 0:
+            first_table[entry] = left_form(value)
+        else:
+            other_table[bases[segment] + entry] = right_form(value)
+
+    for level in range(DEPTH):
+        for segment, (origin, size) in enumerate(segments):
+            if level >= size:
+                continue
+            site = origin + level
+            if level == 0 and segment > 0:
+                for bit in range(2):
+                    value = tensors_ref[0, site, bit].astype(jnp.float32)
+                    put(segment, size, 1, bit, value)
+                continue
+            if level == 0:
+                put(segment, size, 0, 0, begin)
+            block = site_weights(tensors_ref[0, site, 0], tensors_ref[0, site, 1])
+            for entry in range(2**level):
+                source = state[segment, pl.ds(entry * chi, chi), :]
+                both = jnp.dot(source, block, preferred_element_type=jnp.float32)
+                put(segment, size, level + 1, entry, both[:, :wide])
+                put(segment, size, level + 1, entry + 2**level, both[:, wide:])
+
     closing_rows[...] = jnp.zeros_like(closing_rows)
 
     def right_copy(piece):
@@ -148,32 +199,23 @@
         base = 0 if at < per else half - per
         return base + group * per + at
 
-    def advance(site, group, final):
-        qubit = order_ref[site]
-        block = weights[site]
-        for at in range(2 * per):
-            where = pl.ds(at * chi, chi)
-            both = jnp.dot(state[where, :], block, preferred_element_type=jnp.float32)
-            item = item_of(group, at)
-            bit = jnp.broadcast_to(bits_ref[item, qubit], (chi, wide))
-            chosen = jnp.where(bit == 1, both[:, wide:], both[:, :wide])
-            if final:
-                mine[item] = chosen
-            else:
-                high, low = split(chosen)
-                state[where, :wide] = high
-                state[where, wide:] = low
-
     def column(group):
         for at in range(2 * per):
-            state[pl.ds(at * chi, chi), :] = start[...]
-
-        def step(site, carry):
-            advance(site, group, False)
-            return carry
-
-        lax.fori_loop(0, sites - 1, step, 0, unroll=UNROLL)
-        advance(sites - 1, group, True)
+            item = item_of(group, at)
+            value = None
+            for segment, (origin, size) in enumerate(segments):
+                entry = bits_ref[item, order_ref[origin]]
+                for level in range(1, size):
+                    bit = bits_ref[item, order_ref[origin + level]]
+                    entry = entry + bit * 2**level
+                if segment == 0:
+                    left = first_table[entry]
+                    continue
+                right = other_table[bases[segment] + entry]
+                value = form_product(left, right)
+                if segment < len(segments) - 1:
+                    left = left_form(value)
+            mine[item] = value
 
     def close(item, row, value):
         edge = right_ref[0]
@@ -240,13 +282,13 @@
                 for at in range(pieces):
                     left_copy(turn * pieces + at).start()
 
-        from_left = turn - col
+        from_left = turn - LAG * col
 
         @pl.when((col > 0) & (from_left >= 0) & (from_left < groups))
         def _():
             merge_right(from_left)
 
-        from_right = turn - (last - col)
+        from_right = turn - LAG * (last - col)
 
         @pl.when((col < last) & (from_right >= 0) & (from_right < groups))
         def _():
@@ -254,7 +296,7 @@
 
         return carry
 
-    lax.fori_loop(0, groups + last, slot, 0)
+    lax.fori_loop(0, groups + LAG * last, slot, 0)
 
     def final_copy(peer, place):
         return pltpu.make_async_remote_copy(
@@ -342,15 +384,16 @@
     vmem = pl.BlockSpec(memory_space=pltpu.VMEM)
     smem = pl.BlockSpec(memory_space=pltpu.SMEM)
     lane_rows = 128
+    sizes = [2**size for _, size in segments_of(sites)]
     return pl.pallas_call(
         functools.partial(kernel, n_col, n_slc, groups, pieces),
         out_shape=jax.ShapeDtypeStruct((2, batch), jnp.float32),
         in_specs=[smem, smem, vmem, vmem, vmem],
         out_specs=vmem,
         scratch_shapes=[
-            pltpu.VMEM((sites, 2 * wide, 2 * wide), jnp.bfloat16),
-            pltpu.VMEM((batch // groups * chi, 2 * wide), jnp.bfloat16),
-            pltpu.VMEM((chi, 2 * wide), jnp.bfloat16),
+            pltpu.VMEM((len(sizes), max(sizes) // 2 * chi, 2 * wide), jnp.bfloat16),
+            pltpu.VMEM((sizes[0], 2 * chi, wide), jnp.bfloat16),
+            pltpu.VMEM((sum(sizes[1:]), 2 * chi, 2 * wide), jnp.bfloat16),
             pltpu.VMEM((batch, chi, wide), jnp.float32),
             pltpu.VMEM((batch, chi, wide), jnp.float32),
             pltpu.VMEM((lane_rows, wide), jnp.float32),

time: 44.5 us -> 38.1 us (0.86)
  Pallas kernels: 43.1 us -> 36.7 us
    pallas_call x1, Pallas kernels: 43.1 us -> 36.7 us  [on_device(): pl.pallas_call(functools.partial(kernel, n_col, n_slc, groups, pieces), o...]
where the time goes in v2:
time: 38.1 us; the launch traced here: 38 us
  Pallas kernels  36.7 us (96%)
  local copies, waits for them, and re-layouts  1.24 us (3%)
    pallas_call x1, Pallas kernels, on_device(): pl.pallas_call(functools.partial(kernel, n_col, n_slc, groups, pieces), o...  36.7 us
    unnamed x1, local copies, waits for them, and re-layouts  1.24 us

profile of v2, /device:TPU:0, one launch (start us, length us, event | category | flops | bytes accessed | tf_op | source)
XLA Modules:
  0.0 38.0 jit_solution(5657448835378799647)
XLA Ops:
  0.0 36.7 %shard_map.55 = f32[2,32]{1,0:T(2,128)} custom-call(s32[18]{0:T(128)} %order_ref.1, s32[32,72]{1,0:T(8,128)} %bits_ref.1, bf16[1,18,2,64,128]{4,3,2,1,0:T(8,128)(2,1)} %tensors_ref.1, f32[1,64,128]{2,1,0:T(8,128)} %left_ref.1, f32[1,64,128]{2,1,0:T(8,128)} %right_ref.1), custom_call_target="tpu_custom_call" | custom-call | tf_op jit(solution)/shard_map/pallas_call | solution.py:388
  36.7 1.2 %copy.7 = f32[2,32]{1,0:T(2,128)} copy(f32[2,32]{1,0:T(2,128)} %shard_map.55) | data formatting | bytes 512

commit v3 on v2

--- a/solution.py
+++ b/solution.py
@@ -10,7 +10,7 @@
 MESH = pl.DeviceIdType.MESH
 GROUPS = 8
 PIECES = 1
-LAG = 2
+LAG = 3
 DEPTH = 5
 
 
@@ -82,10 +82,14 @@
     pieces,
     order_ref,
     bits_ref,
+    tensors_hbm,
+    left_hbm,
+    right_hbm,
+    out_ref,
     tensors_ref,
     left_ref,
     right_ref,
-    out_ref,
+    load_sem,
     state,
     first_table,
     other_table,
@@ -115,19 +119,29 @@
 
     barrier = pltpu.get_barrier_semaphore()
 
-    def greet(peer, carry):
-        @pl.when(peer != me)
-        def _():
-            pl.semaphore_signal(
-                barrier,
-                inc=1,
-                device_id={"col": peer // n_slc, "slc": lax.rem(peer, n_slc)},
-                device_id_type=MESH,
-            )
-
-        return carry
-
-    lax.fori_loop(0, peers, greet, 0)
+    def greet(where):
+        pl.semaphore_signal(barrier, inc=1, device_id=where, device_id_type=MESH)
+
+    @pl.when(col > 0)
+    def _():
+        greet({"col": lax.rem(col + last, n_col)})
+
+    @pl.when(col < last)
+    def _():
+        greet({"col": lax.rem(col + 1, n_col)})
+
+    for step in range(1, n_slc):
+        greet({"slc": lax.rem(slc + step, n_slc)})
+
+    loads = [
+        pltpu.make_async_copy(tensors_hbm, tensors_ref, load_sem.at[0]),
+        pltpu.make_async_copy(left_hbm, left_ref, load_sem.at[1]),
+        pltpu.make_async_copy(right_hbm, right_ref, load_sem.at[2]),
+    ]
+    for load in loads:
+        load.start()
+    for load in loads:
+        load.wait()
 
     rows = lax.broadcasted_iota(jnp.int32, (chi, wide), 0)
     lanes = lax.broadcasted_iota(jnp.int32, (chi, wide), 1)
@@ -200,21 +214,26 @@
         return base + group * per + at
 
     def column(group):
-        for at in range(2 * per):
-            item = item_of(group, at)
-            value = None
-            for segment, (origin, size) in enumerate(segments):
-                entry = bits_ref[item, order_ref[origin]]
+        items = [item_of(group, at) for at in range(2 * per)]
+        values = []
+        for segment, (origin, size) in enumerate(segments):
+            qubits = [order_ref[origin + level] for level in range(size)]
+            entries_of = []
+            for item in items:
+                entry = bits_ref[item, qubits[0]]
                 for level in range(1, size):
-                    bit = bits_ref[item, order_ref[origin + level]]
-                    entry = entry + bit * 2**level
-                if segment == 0:
-                    left = first_table[entry]
-                    continue
-                right = other_table[bases[segment] + entry]
-                value = form_product(left, right)
-                if segment < len(segments) - 1:
-                    left = left_form(value)
+                    entry = entry + bits_ref[item, qubits[level]] * 2**level
+                entries_of.append(entry)
+            if segment == 0:
+                lefts = [first_table[entry] for entry in entries_of]
+                continue
+            if segment > 1:
+                lefts = [left_form(value) for value in values]
+            values = [
+                form_product(left, other_table[bases[segment] + entry])
+                for left, entry in zip(lefts, entries_of)
+            ]
+        for item, value in zip(items, values):
             mine[item] = value
 
     def close(item, row, value):
@@ -231,9 +250,10 @@
         for piece_at in range(pieces):
             piece = group * pieces + piece_at
             right_copy(piece).wait_recv()
-            for at in range(chunk):
-                item = piece * chunk + at
-                mine[item] = complex_product(arrived[item], mine[item])
+            items = [piece * chunk + at for at in range(chunk)]
+            values = [complex_product(arrived[item], mine[item]) for item in items]
+            for item, value in zip(items, values):
+                mine[item] = value
 
             @pl.when(col < last)
             def _():
@@ -249,9 +269,10 @@
         for piece_at in range(pieces):
             piece = group * pieces + piece_at
             left_copy(piece).wait_recv()
-            for at in range(chunk):
-                item = half + piece * chunk + at
-                mine[item] = complex_product(mine[item], arrived[item])
+            items = [half + piece * chunk + at for at in range(chunk)]
+            values = [complex_product(mine[item], arrived[item]) for item in items]
+            for item, value in zip(items, values):
+                mine[item] = value
 
             @pl.when(col > 0)
             def _():
@@ -270,7 +291,8 @@
 
             @pl.when(turn == 0)
             def _():
-                pl.semaphore_wait(barrier, peers - 1)
+                near = jnp.where((col > 0) & (col < last), 2, 1)
+                pl.semaphore_wait(barrier, near + n_slc - 1)
 
             @pl.when(col == 0)
             def _():
@@ -383,14 +405,19 @@
     chunks = groups * pieces
     vmem = pl.BlockSpec(memory_space=pltpu.VMEM)
     smem = pl.BlockSpec(memory_space=pltpu.SMEM)
+    hbm = pl.BlockSpec(memory_space=pl.ANY)
     lane_rows = 128
     sizes = [2**size for _, size in segments_of(sites)]
     return pl.pallas_call(
         functools.partial(kernel, n_col, n_slc, groups, pieces),
         out_shape=jax.ShapeDtypeStruct((2, batch), jnp.float32),
-        in_specs=[smem, smem, vmem, vmem, vmem],
+        in_specs=[smem, smem, hbm, hbm, hbm],
         out_specs=vmem,
         scratch_shapes=[
+            pltpu.VMEM(site_tensors.shape, site_tensors.dtype),
+            pltpu.VMEM(left_edge.shape, left_edge.dtype),
+            pltpu.VMEM(right_edge.shape, right_edge.dtype),
+            pltpu.SemaphoreType.DMA((3,)),
             pltpu.VMEM((len(sizes), max(sizes) // 2 * chi, 2 * wide), jnp.bfloat16),
             pltpu.VMEM((sizes[0], 2 * chi, wide), jnp.bfloat16),
             pltpu.VMEM((sum(sizes[1:]), 2 * chi, 2 * wide), jnp.bfloat16),

time: 38.1 us -> 36 us (0.945)
  Pallas kernels: 36.7 us -> 34.4 us
    pallas_call x1, Pallas kernels: 36.7 us -> 34.4 us  [on_device(): pl.pallas_call(functools.partial(kernel, n_col, n_slc, groups, pieces), o...]
where the time goes in v3:
time: 36 us; the launch traced here: 35.7 us
  Pallas kernels  34.4 us (96%)
  local copies, waits for them, and re-layouts  1.24 us (3%)
    pallas_call x1, Pallas kernels, on_device(): pl.pallas_call(functools.partial(kernel, n_col, n_slc, groups, pieces), o...  34.4 us
    unnamed x1, local copies, waits for them, and re-layouts  1.24 us

profile of v3, /device:TPU:0, one launch (start us, length us, event | category | flops | bytes accessed | tf_op | source)
XLA Modules:
  0.0 35.7 jit_solution(15425979775211498281)
XLA Ops:
  0.0 34.4 %shard_map.55 = f32[2,32]{1,0:T(2,128)} custom-call(s32[18]{0:T(128)} %order_ref.1, s32[32,72]{1,0:T(8,128)} %bits_ref.1, bf16[1,18,2,64,128]{4,3,2,1,0:T(8,128)(2,1)} %tensors_hbm.1, f32[1,64,128]{2,1,0:T(8,128)} %left_hbm.1, f32[1,64,128]{2,1,0:T(8,128)} %right_hbm.1), custom_call_target="tpu_custom_call" | custom-call | tf_op jit(solution)/shard_map/pallas_call | solution.py:411
  34.5 1.2 %copy.7 = f32[2,32]{1,0:T(2,128)} copy(f32[2,32]{1,0:T(2,128)} %shard_map.55) | data formatting | bytes 512
